TPU v7x, 32 devices: a whole 2x2x4 slice. The times are simulated.
32 devices in a mesh: z: 4 (over z), y: 2 (over y), x: 4 (over x, core).
Axes of the slice: x: 2, y: 2, z: 4, core: 2. Of those that a mesh axis runs over, the one named last changes fastest.
Arguments:
- atom_pos: float32 [23328, 3], P(('z', 'y', 'x'))
- atom_vel: float32 [23328, 3], P(('z', 'y', 'x'))
- atom_frc: float32 [23328, 3], P(('z', 'y', 'x'))
- atom_id: int32 [23328], P(('z', 'y', 'x'))
- atom_ok: int32 [23328], P(('z', 'y', 'x'))
- brick_side: float32 [], replicated
Outputs:
- output 1: float32 [23328, 3], P(('z', 'y', 'x'))
- output 2: float32 [23328, 3], P(('z', 'y', 'x'))
- output 3: float32 [23328, 3], P(('z', 'y', 'x'))
- output 4: int32 [23328], P(('z', 'y', 'x'))
- output 5: int32 [23328], P(('z', 'y', 'x'))
- output 6: float32 [], replicated
All inputs are finite; a program needn't handle non-finite values.
Results may differ from a plain program's by a relative error of at most 0.001.
Values sent between devices are 32-bit elements.
A program may use at most 1 GiB of HBM per device.

v0:
```python
import functools

import jax
import jax.numpy as jnp
from jax import lax
from jax.experimental import pallas as pl
from jax.experimental.pallas import tpu as pltpu
from jax.sharding import PartitionSpec as P

DT = 0.005
RC = 2.5
FAR = 1.0e6
UCUT = 4.0 * (RC ** -12 - RC ** -6)
UPC = -48.0 * RC ** -13 + 24.0 * RC ** -7
MESH_AXES = ("z", "y", "x")
DIRS = [(dx, dy, dz) for dz in (-1, 0, 1) for dy in (-1, 0, 1) for dx in (-1, 0, 1) if (dx, dy, dz) != (0, 0, 0)]
NEAR = RC + 1.0e-3
MAJOR = ((2, 1, 0), (1, 0, 2), (0, 2, 1))
PACK = 8
NEW = 256
CHUNK = 3
GROUPS = 8
L = 128
TILE = (8, L)
F32 = jnp.float32
BF16 = jnp.bfloat16
I32 = jnp.int32
NT = (((1,), (1,)), ((), ()))
NN = (((1,), (0,)), ((), ()))


def device_of(sizes, me, offset):
    return tuple(lax.rem(me[axis] + offset[axis], sizes[axis]) for axis in (2, 1, 0))


def offset_of(sizes, d):
    return tuple(c % size for c, size in zip(d, sizes))


def order_of(d):
    if d[2] == 0:
        return 1 if d[1] != 0 else 2
    return 2 if (d[1] == 0 and d[0] != 0) else 0


def range_of(d):
    first, size = 0, 27
    for axis in MAJOR[order_of(d)]:
        if d[axis] == 0:
            break
        size = size // 3
        first = first + (1, 0, 2)[d[axis]] * size
    return first, first + size


def split3(x):
    hi = x.astype(BF16)
    rest = x - hi.astype(F32)
    mid = rest.astype(BF16)
    low = (rest - mid.astype(F32)).astype(BF16)
    return hi, mid, low


def onehot_rows(dest, base, count):
    rows = lax.broadcasted_iota(I32, (count, dest.shape[1]), 0) + base
    return jnp.where(rows == dest, 1.0, 0.0).astype(BF16)


def scatter_lanes(data, dest, slots):
    rows = data.shape[0]
    parts = jnp.concatenate(split3(data), axis=0)
    out = []
    for base in range(0, slots, 256):
        hot = onehot_rows(dest, base, min(256, slots - base))
        got = lax.dot_general(parts, hot, NT, preferred_element_type=F32)
        out.append(got[0:rows] + got[rows:2 * rows] + got[2 * rows:3 * rows])
    return jnp.concatenate(out, axis=1)


def class_places(code, with_before):
    width = code.shape[1]
    tiles = width // L
    cls = lax.broadcasted_iota(I32, (32, width), 0)
    member = jnp.where(cls == code, 1.0, 0.0)
    member_b = member.astype(BF16)
    stacked = jnp.concatenate([member_b[:, t * L:(t + 1) * L] for t in range(tiles)], axis=0)
    row_i = lax.broadcasted_iota(I32, (L, 256), 0)
    col_i = lax.broadcasted_iota(I32, (L, 256), 1)
    tri = jnp.where((row_i < col_i) | (col_i >= L), 1.0, 0.0).astype(BF16)
    pre = lax.dot_general(stacked, tri, NN, preferred_element_type=F32)
    carry = jnp.zeros((32, L), F32)
    if with_before:
        before_b = jnp.where(code < cls, 1.0, 0.0).astype(BF16)
        before_s = before_b[:, 0:L]
        tot = None
        ones = jnp.ones((L, L), BF16)
        for t in range(tiles):
            part = lax.dot_general(before_b[:, t * L:(t + 1) * L], ones, NN, preferred_element_type=F32)
            tot = part if tot is None else tot + part
        before = tot
        carry = before
    else:
        before = None
    places = []
    for t in range(tiles):
        within = pre[32 * t:32 * t + 32, 0:L] + carry
        places.append(jnp.sum(member[:, t * L:(t + 1) * L] * within, axis=0, keepdims=True))
        carry = carry + pre[32 * t:32 * t + 32, L:256]
    return jnp.concatenate(places, axis=1), before


def pad_lanes(x, width):
    return jnp.concatenate([x, jnp.zeros((x.shape[0], width - x.shape[1]), x.dtype)], axis=1)


def pair_loop(own_cols, near_lanes, q, first, last, with_self, carry):
    rows = [step_rows(q, g) for g in range(GROUPS)]
    own = [[own_cols[rows[g], a * L:(a + 1) * L] for a in range(3)] for g in range(GROUPS)]

    def body(c, carry):
        force, en = [list(f) for f in carry[0]], list(carry[1])
        for t in range(CHUNK):
            place = pl.ds(pl.multiple_of((c * CHUNK + t) * L, L), L)
            near_xyz = [near_lanes[a, :, place] for a in range(3)]
            for g in range(GROUPS):
                dx, dy, dz = [own[g][a] - near_xyz[a] for a in range(3)]
                d2 = dx * dx + dy * dy + dz * dz
                near = d2 < RC * RC
                if with_self:
                    near = near & (d2 > 0.0)
                inv = jnp.where(near, lax.rsqrt(d2), 0.0)
                s2 = inv * inv
                s6 = s2 * s2 * s2
                s12 = s6 * s6
                p = s12 - s6
                w = inv * (UPC / 24.0)
                scale = (p + s12) * s2 + w
                en = [en[0] + p, en[1] + w * d2, en[2] + jnp.where(near, 1.0, 0.0)]
                force[g] = [force[g][0] + scale * dx, force[g][1] + scale * dy, force[g][2] + scale * dz]
        return tuple(tuple(f) for f in force), tuple(en)

    return lax.fori_loop(first, last, body, carry)


def step_rows(q, g):
    return pl.ds(pl.multiple_of((q * GROUPS + g) * 8, 8), 8)


def own_columns(xyz):
    slots = xyz.shape[1]
    parts = [part.astype(F32) for part in split3(xyz)]
    parts = jnp.concatenate(parts + [jnp.zeros((7, slots), F32)], axis=0)
    row = lax.broadcasted_iota(I32, (16, 3 * L), 0)
    tile = lax.broadcasted_iota(I32, (16, 3 * L), 1) // L
    picks = jnp.where((row == tile) | (row == tile + 3) | (row == tile + 6), 1.0, 0.0).astype(BF16)
    return lax.dot_general(jnp.transpose(parts).astype(BF16), picks, NN, preferred_element_type=F32)


def exchange_kernel(sizes, peers, slots, pos_hbm, vel_hbm, frc_hbm, id_hbm, ok_hbm, side_ref, srt_ref, gh_ref, ga_ref, own_ref, inner_ref, inner_en_ref, pos_ref, vel_ref, frc_ref, id_ref, ok_ref, pkt, rcv, out3, new3, lanes, isem, psend, precv, gsend, grecv, asend, arecv):
    me = [lax.axis_index(name) for name in "xyz"]

    device_at = functools.partial(device_of, sizes, me)

    loads = []
    for index, (src, dst) in enumerate(((ok_hbm, ok_ref), (id_hbm, id_ref), (pos_hbm, pos_ref), (vel_hbm, vel_ref), (frc_hbm, frc_ref))):
        load = pltpu.make_async_copy(src, dst, isem.at[index])
        load.start()
        loads.append(load)
    barrier = pltpu.get_barrier_semaphore()
    for offset in peers:
        pl.semaphore_signal(barrier, inc=1, device_id=device_at(offset), device_id_type=pl.DeviceIdType.MESH)

    n = pos_ref.shape[1]
    for load in loads:
        load.wait()
    side = side_ref[0, 0]
    owned = pad_lanes(jnp.reshape(ok_ref[...], (1, n)), slots) > 0
    half = vel_ref[...] + (0.5 * DT) * frc_ref[...]
    free = pos_ref[...] + DT * half
    half = pad_lanes(half, slots)
    free = pad_lanes(free, slots)
    ids = pad_lanes(jnp.reshape(id_ref[...], (1, n)), slots)
    code = jnp.zeros((1, slots), I32)
    moved = []
    low_side = []
    for axis in range(3):
        low = me[axis].astype(F32) * side
        high = (me[axis] + 1).astype(F32) * side
        box = side * float(sizes[axis])
        u = free[axis:axis + 1]
        step = jnp.where(u >= high, 1, 0) - jnp.where(u < low, 1, 0)
        code = code + (step + 1) * (1, 3, 9)[axis]
        moved.append(jnp.where(u < 0.0, u + box, jnp.where(u >= box, u - box, u)))
        low_side.append(low)
    code = jnp.where(owned, code, 31)
    id_hi = (ids >> 16).astype(F32)
    id_lo = (ids & 65535).astype(F32)
    okf = jnp.where(owned, 1.0, 0.0)
    data = jnp.concatenate(moved + [half, id_hi, id_lo, okf, jnp.zeros((7, slots), F32)], axis=0)

    place, _ = class_places(code, False)
    leaving = owned & (code != 13)
    way = jnp.where(leaving, code - jnp.where(code > 13, 1, 0), 31)
    member = jnp.where(lax.broadcasted_iota(I32, (32, slots), 0) == way, 1.0, 0.0).astype(BF16)
    fields = jnp.concatenate([jnp.where(place == float(k), data, 0.0) for k in range(PACK)], axis=0)
    packed = jnp.zeros((32, L), F32)
    for part in split3(fields):
        packed = packed + lax.dot_general(member, part, NT, preferred_element_type=F32)
    pkt[...] = packed

    def bins_of(pos):
        bins = []
        for axis in range(3):
            loc = pos[axis:axis + 1] - low_side[axis]
            bins.append(jnp.where(loc < NEAR, 0, jnp.where(loc > side - NEAR, 2, 1)))
        return [(bins[i] * 3 + bins[j]) * 3 + bins[k] for i, j, k in MAJOR]

    wide = side > 2.0 * NEAR
    eye = lax.broadcasted_iota(I32, (32, L), 0) == lax.broadcasted_iota(I32, (32, L), 1)

    def sorted_block(cand, keys, kept):
        width = cand.shape[1]
        where_to, before = class_places(jnp.where(kept, keys, 28), True)
        arranged = scatter_lanes(cand, jnp.where(kept, where_to.astype(I32), -1), width)
        total = jnp.concatenate([before[27:28]] * (width // L), axis=1)
        lane = lax.broadcasted_iota(I32, (1, width), 1).astype(F32)
        begins = jnp.sum(jnp.where(eye, before, 0.0), axis=0, keepdims=True)
        ends = jnp.where(wide, begins, before[27:28])
        counts = jnp.concatenate([jnp.where(wide, begins, 0.0)[:, 0:32], ends[:, 0:32], jnp.zeros((1, L - 64), F32)], axis=1)
        return jnp.concatenate([jnp.where(lane < total, arranged[0:3], FAR), pad_lanes(counts, width)], axis=0)

    def send(src, dst, ssem, rsem, offset):
        copy = pltpu.make_async_remote_copy(
            src_ref=src, dst_ref=dst, send_sem=ssem, recv_sem=rsem,
            device_id=device_at(offset), device_id_type=pl.DeviceIdType.MESH)
        copy.start()
        return copy

    def send_blocks(block, dst, ssem, rsem, kind):
        out = []
        for index, offset in enumerate(peers):
            if order_of(tuple(0 if c == 0 else 1 for c in offset)) == kind:
                out.append(send(block.at[kind], dst.at[index], ssem.at[index], rsem.at[index], offset))
        return out

    staying = code == 13
    keys = bins_of(data)
    for kind in range(3):
        out3[kind] = sorted_block(data[0:8], keys[kind], staying)
    pl.semaphore_wait(barrier, len(peers))
    packets = []
    for index, d in enumerate(DIRS):
        row = pl.ds(index, 1)
        packets.append(send(pkt.at[row], rcv.at[row], psend.at[index], precv.at[index], offset_of(sizes, d)))
    blocks = []
    for kind in range(3):
        blocks = blocks + send_blocks(out3, gh_ref, gsend, grecv, kind)
    for copy in packets:
        copy.wait_recv()

    came = jnp.concatenate([rcv[...], jnp.zeros((32 - 26, L), F32)], axis=0)
    came = jnp.concatenate([came] + [pltpu.roll(came, L - 16 * k, 1) for k in range(1, PACK)], axis=0)
    came_t = jnp.transpose(came)[0:16]
    came_ok = came_t[8:9] > 0.5
    keys = bins_of(came_t)
    late = []
    for kind in range(3):
        new3[kind] = sorted_block(came_t[0:8], keys[kind], came_ok)
        late = late + send_blocks(new3, ga_ref, asend, arecv, kind)
    for copy in packets:
        copy.wait_send()

    arr_ids = came[:, 6:7].astype(I32) * 65536 + came[:, 7:8].astype(I32)
    arr_ok = came[:, 8:9] > 0.5
    row_ids = jnp.concatenate([ids, came_t[6:7].astype(I32) * 65536 + came_t[7:8].astype(I32)], axis=1)
    less = jnp.where((arr_ids < row_ids) & arr_ok, 1.0, 0.0)
    arrivals_below = jnp.sum(less, axis=0, keepdims=True)
    above = jnp.where((arr_ids > row_ids[:, 0:slots]) & staying, 1.0, 0.0).astype(BF16)
    stay_below = lax.dot_general(jnp.ones((16, slots), BF16), above, NT, preferred_element_type=F32)[0:1]
    stay_place, _ = class_places(jnp.where(staying, 0, 31), False)
    rank = jnp.concatenate([stay_place, stay_below], axis=1) + arrivals_below
    dest = jnp.where(jnp.concatenate([staying, came_ok], axis=1), rank.astype(I32), -1)
    merged = scatter_lanes(jnp.concatenate([data, came_t], axis=1), dest, slots)
    srt_ref[...] = jnp.where(lax.broadcasted_iota(I32, (16, slots), 0) == 9, side, merged)

    good = merged[8:9] > 0.5
    own_ref[...] = own_columns(jnp.where(good, merged[0:3], -FAR))
    first = CHUNK * L
    for a in range(3):
        lanes[a] = jnp.broadcast_to(jnp.where(good, merged[a:a + 1], FAR)[:, 0:first], (8, first))
    zero = jnp.zeros(TILE, F32)

    def own_step(q, energy):
        force, energy = pair_loop(own_ref, lanes, q, 0, 1, True, (((zero,) * 3,) * GROUPS, energy))
        for g in range(GROUPS):
            for a in range(3):
                inner_ref[a, step_rows(q, g), :] = force[g][a]
        return energy

    for k, part in enumerate(lax.fori_loop(0, slots // (8 * GROUPS), own_step, (zero,) * 3)):
        inner_en_ref[k] = part

    for copy in blocks + late:
        copy.wait()


def force_kernel(sizes, peers, slots, srt_ref, gh_ref, ga_ref, own_cols, inner_ref, inner_en_ref, offs_ref, pos_ref, vel_ref, frc_ref, id_ref, ok_ref, en_ref, line, wide_line, sums, added):
    me = [lax.axis_index(name) for name in "xyz"]
    n = pos_ref.shape[1]
    side = srt_ref[9:10, 0:1]
    okrow = srt_ref[8:9]
    good = okrow > 0.5
    count = jnp.sum(okrow).astype(I32)
    span = slots + L

    away = jnp.full(TILE, FAR, F32)
    first = CHUNK * L
    line[:, 0:slots - first] = jnp.concatenate([jnp.where(good, srt_ref[0:3], FAR), jnp.full((5, slots), FAR, F32)], axis=0)[:, first:]
    lane = lax.broadcasted_iota(I32, (8, span), 1)
    fill = jnp.maximum(count - first, 0)
    for d in DIRS:
        index = peers.index(offset_of(sizes, [-c for c in d]))
        low, high = range_of(d)
        shifts = []
        for axis in range(3):
            box = side * float(sizes[axis])
            if d[axis] == 1:
                shifts.append(jnp.where(me[axis] == sizes[axis] - 1, box, 0.0))
            elif d[axis] == -1:
                shifts.append(jnp.where(me[axis] == 0, -box, 0.0))
            else:
                shifts.append(jnp.zeros((1, 1), F32))
        for source, entry in ((gh_ref, index), (ga_ref, index + len(peers))):
            width = source.shape[2]
            begin = offs_ref[entry, low]
            end = offs_ref[entry, 32 + high]
            block = jnp.concatenate([source[index, a:a + 1] + shifts[a] for a in range(3)] + [jnp.zeros((5, width), F32)], axis=0)
            block = jnp.concatenate([block, away], axis=1)
            head = fill & (L - 1)
            base = pl.multiple_of(fill - head, L)
            move = head - begin
            block = pltpu.roll(block, jnp.where(move < 0, move + (width + L), move), 1)
            block = jnp.where(lane[:, 0:width + L] < head + end - begin, block, FAR)
            line[:, pl.ds(base, L)] = jnp.where(lane[:, 0:L] < head, line[:, pl.ds(base, L)], block[:, 0:L])
            line[:, pl.ds(pl.multiple_of(base + L, L), width)] = block[:, L:]
            fill = fill + (end - begin)
    rest = pl.multiple_of(((fill + L - 1) // L) * L, L)
    line[:, pl.ds(rest, CHUNK * L)] = jnp.full((8, CHUNK * L), FAR, F32)
    chunks = jnp.maximum((fill + CHUNK * L - 1) // (CHUNK * L), 1)

    def widen(c, carry):
        for t in range(CHUNK):
            place = pl.ds(pl.multiple_of((c * CHUNK + t) * L, L), L)
            tile = line[:, place]
            for a in range(3):
                wide_line[a, :, place] = jnp.broadcast_to(tile[a:a + 1], TILE)
        return carry

    lax.fori_loop(0, chunks, widen, 0)

    def own_step(q, energy):
        start = tuple(tuple(inner_ref[a, step_rows(q, g), :] for a in range(3)) for g in range(GROUPS))
        carry = pair_loop(own_cols, wide_line, q, 0, 1, True, (start, energy))
        force, energy = pair_loop(own_cols, wide_line, q, 1, chunks, False, carry)
        for g in range(GROUPS):
            for a in range(3):
                sums[a, step_rows(q, g), :] = force[g][a]
        return energy

    own_steps = (count + 8 * GROUPS - 1) // (8 * GROUPS)
    energy = lax.fori_loop(0, own_steps, own_step, tuple(inner_en_ref[k] for k in range(3)))
    en_ref[...] = jnp.sum(2.0 * energy[0] - 12.0 * energy[1] + 0.5 * (RC * UPC - UCUT) * energy[2], axis=0, keepdims=True)

    col = lax.broadcasted_iota(I32, (L, L), 1)
    picks = [jnp.where(col == a, 1.0, 0.0).astype(BF16) for a in range(3)]

    def add_up(base):
        total = jnp.zeros((2 * L, L), F32)
        for a in range(3):
            for part in split3(sums[a, base:base + 2 * L, :]):
                total = total + lax.dot_general(part, picks[a], NN, preferred_element_type=F32)
        added[:, base:base + 2 * L] = jnp.transpose(total)[0:8]

    for base in range(0, slots, 2 * L):
        pl.when(count > base)(functools.partial(add_up, base))
    force = jnp.where(good, 24.0 * added[0:3], 0.0)
    pos_ref[...] = srt_ref[0:3, 0:n]
    frc_ref[...] = force[:, 0:n]
    vel_ref[...] = (srt_ref[3:6] + (0.5 * DT) * force)[:, 0:n]
    id_ref[...] = jnp.reshape((srt_ref[6:7].astype(I32) * 65536 + srt_ref[7:8].astype(I32))[:, 0:n], (n,))
    ok_ref[...] = jnp.reshape(okrow[:, 0:n].astype(I32), (n,))


def total_kernel(sizes, part_ref, sum_ref, rows, ssem, rsem):
    me = [lax.axis_index(name) for name in "xyz"]
    size_x, size_y, size_z = sizes
    mine = (me[2] * size_y + me[1]) * size_x + me[0]
    others = [(dx, dy, dz) for dz in range(size_z) for dy in range(size_y) for dx in range(size_x) if dx + dy + dz > 0]
    others.sort(key=lambda o: -(2 * min(o[2], size_z - o[2]) + 2 * o[1] + min(o[0], size_x - o[0])))

    device_at = functools.partial(device_of, sizes, me)

    barrier = pltpu.get_barrier_semaphore()
    for offset in others:
        pl.semaphore_signal(barrier, inc=1, device_id=device_at(offset), device_id_type=pl.DeviceIdType.MESH)
    rows[pl.ds(mine, 1)] = part_ref[...]
    pl.semaphore_wait(barrier, len(others))
    copies = []
    for index, offset in enumerate(others):
        copy = pltpu.make_async_remote_copy(
            src_ref=part_ref, dst_ref=rows.at[pl.ds(mine, 1)], send_sem=ssem.at[index], recv_sem=rsem.at[index],
            device_id=device_at(offset), device_id_type=pl.DeviceIdType.MESH)
        copy.start()
        copies.append(copy)
    for copy in copies:
        copy.wait_recv()
    sum_ref[...] = jnp.sum(rows[...], axis=0, keepdims=True)
    for copy in copies:
        copy.wait_send()


def solution(mesh):
    sizes = (mesh.shape["x"], mesh.shape["y"], mesh.shape["z"])
    peers = sorted({offset_of(sizes, d) for d in DIRS} - {(0, 0, 0)})
    devices = sizes[0] * sizes[1] * sizes[2]

    def local_step(atom_pos, atom_vel, atom_frc, atom_id, atom_ok, brick_side):
        n = atom_pos.shape[0]
        slots = -(-n // L) * L
        side = jnp.reshape(brick_side, (1, 1))
        vmem = pl.BlockSpec(memory_space=pltpu.VMEM)
        smem = pl.BlockSpec(memory_space=pltpu.SMEM)
        srt, ghosts, fresh, own, inner, inner_en = pl.pallas_call(
            functools.partial(exchange_kernel, sizes, peers, slots),
            out_shape=(jax.ShapeDtypeStruct((16, slots), F32), jax.ShapeDtypeStruct((len(peers), 4, slots), F32), jax.ShapeDtypeStruct((len(peers), 4, NEW), F32),
                       jax.ShapeDtypeStruct((slots, 3 * L), F32), jax.ShapeDtypeStruct((3, slots, L), F32), jax.ShapeDtypeStruct((3,) + TILE, F32)),
            in_specs=[pl.BlockSpec(memory_space=pltpu.HBM)] * 5 + [smem],
            out_specs=(vmem,) * 6,
            scratch_shapes=[
                pltpu.VMEM((3, n), F32), pltpu.VMEM((3, n), F32), pltpu.VMEM((3, n), F32), pltpu.VMEM((n,), I32), pltpu.VMEM((n,), I32),
                pltpu.VMEM((32, L), F32), pltpu.VMEM((26, L), F32), pltpu.VMEM((3, 4, slots), F32), pltpu.VMEM((3, 4, NEW), F32), pltpu.VMEM((3, 8, CHUNK * L), F32),
                pltpu.SemaphoreType.DMA((5,)), pltpu.SemaphoreType.DMA((26,)), pltpu.SemaphoreType.DMA((26,)),
            ] + [pltpu.SemaphoreType.DMA((len(peers),))] * 4,
            compiler_params=pltpu.CompilerParams(collective_id=0, has_side_effects=True, vmem_limit_bytes=40 * 2 ** 20),
            name="exchange",
        )(*[pltpu.with_memory_space_constraint(v, pltpu.HBM) for v in (atom_pos.T, atom_vel.T, atom_frc.T, atom_id, atom_ok)], side)
        offs = jnp.concatenate([ghosts[:, 3, 0:64], fresh[:, 3, 0:64]], axis=0).astype(I32)
        out_f = jax.ShapeDtypeStruct((3, n), F32)
        out_i = jax.ShapeDtypeStruct((n,), I32)
        new_pos, new_vel, new_frc, new_id, new_ok, energy = pl.pallas_call(
            functools.partial(force_kernel, sizes, peers, slots),
            out_shape=(out_f, out_f, out_f, out_i, out_i, jax.ShapeDtypeStruct((1, L), F32)),
            in_specs=[vmem] * 6 + [smem],
            out_specs=(vmem,) * 6,
            scratch_shapes=[pltpu.VMEM((8, 28 * slots + CHUNK * L), F32), pltpu.VMEM((3, 8, 28 * slots + CHUNK * L), F32), pltpu.VMEM((3, slots, L), F32), pltpu.VMEM((8, slots), F32)],
            compiler_params=pltpu.CompilerParams(vmem_limit_bytes=40 * 2 ** 20),
            name="forces",
        )(srt, ghosts, fresh, own, inner, inner_en, offs)
        energy = pl.pallas_call(
            functools.partial(total_kernel, sizes),
            out_shape=jax.ShapeDtypeStruct((1, L), F32),
            in_specs=[vmem],
            out_specs=vmem,
            scratch_shapes=[pltpu.VMEM((devices, L), F32), pltpu.SemaphoreType.DMA((devices,)), pltpu.SemaphoreType.DMA((devices,))],
            compiler_params=pltpu.CompilerParams(collective_id=1, has_side_effects=True, vmem_limit_bytes=4 * 2 ** 20),
            name="total",
        )(pltpu.with_memory_space_constraint(energy, pltpu.VMEM))
        return new_pos.T, new_vel.T, new_frc.T, new_id, new_ok, jnp.sum(energy)

    row_spec = P(MESH_AXES, None)
    id_spec = P(MESH_AXES)
    return jax.shard_map(local_step, mesh=mesh, in_specs=(row_spec, row_spec, row_spec, id_spec, id_spec, P()), out_specs=(row_spec, row_spec, row_spec, id_spec, id_spec, P()), check_vma=False)
```

profile of v0, /device:TPU:0, one launch (start us, length us, event | category | flops | bytes accessed | tf_op | source)
XLA Modules:
  0.0 33.0 jit_solution(1339523477314317374)
XLA Ops:
  1.3 16.5 %exchange.1 = (f32[16,768]{1,0:T(8,128)S(1)}, f32[17,4,768]{2,1,0:T(4,128)S(1)}, f32[17,4,256]{2,1,0:T(4,128)S(1)}, f32[768,384]{1,0:T(8,128)S(1)}, f32[3,768,12...) custom-call(f32[3,729]{1,0:T(4,128)} %bitcast.12, f32[3,729]{1,0:T(4,128)} %bitcast.13, f32[3,729]{1,0:T(4,128)} %bitcast.14, ...), custom_call_target="tpu_custom_call" | custom-call | tf_op jit(solution)/shard_map/exchange/pallas_call | solution.py:433
  17.9 5.3 %forces.1 = (f32[3,729]{1,0:T(4,128)}, f32[3,729]{1,0:T(4,128)}, f32[3,729]{1,0:T(4,128)}, s32[729]{0:T(1024)}, s32[729]{0:T(1024)}, /*index=5*/f32[1,128]{1,0:T(1,128)S(1)}) custom-call(f32[16,768]{1,0:T(8,128)S(1)} %get-tuple-element.18.srt_ref, f32[17,4,768]{2,1,0:T(4,128)S(1)} %get-tuple-element.19.gh_ref, f32[17,4,256]{2,1,0:T(4,128)S(1)} %get-tuple-element.20.ga_ref, ...), custom_call_target="tpu_custom_call" | custom-call | tf_op jit(solution)/shard_map/forces/pallas_call | solution.py:450
  23.2 9.2 %total.1 = f32[1,128]{1,0:T(1,128)S(1)} custom-call(f32[1,128]{1,0:T(1,128)S(1)} %get-tuple-element.29.part_ref), custom_call_target="tpu_custom_call" | custom-call | tf_op jit(solution)/shard_map/total/pallas_call | solution.py:459
  32.4 0.6 %reduce_sum.9 = f32[]{:T(128)} reduce(f32[1,128]{1,0:T(1,128)S(1)} %total.1, f32[]{:T(128)} %constant.0.clone.1), dimensions={0,1}, to_apply=%region_0.0 | reduce | flops 127 | bytes 520 | tf_op jit(solution)/shard_map/reduce_sum | solution.py:468
  (4 shorter events, 0.1 us)
where the time goes:
time: 33 us
  Pallas kernels  31 us (94%)
  between operations  1.33 us (4%)
  other arithmetic  0.61 us (2%)
    pallas_call x1, Pallas kernels, local_step(): pl.pallas_call(functools.partial(exchange_kernel, sizes, peers, slots), o...  16.5 us
    pallas_call x1, Pallas kernels, local_step(): pl.pallas_call(functools.partial(total_kernel, sizes), out_shape=jax.Shap...  9.21 us
    pallas_call x1, Pallas kernels, local_step(): pl.pallas_call(functools.partial(force_kernel, sizes, peers, slots), out_...  5.29 us

commit v1 on v0

--- a/solution.py
+++ b/solution.py
@@ -227,7 +227,7 @@
         begins = jnp.sum(jnp.where(eye, before, 0.0), axis=0, keepdims=True)
         ends = jnp.where(wide, begins, before[27:28])
         counts = jnp.concatenate([jnp.where(wide, begins, 0.0)[:, 0:32], ends[:, 0:32], jnp.zeros((1, L - 64), F32)], axis=1)
-        return jnp.concatenate([jnp.where(lane < total, arranged[0:3], FAR), pad_lanes(counts, width)], axis=0)
+        return jnp.where(lane < total, arranged[0:3], FAR), counts
 
     def send(src, dst, ssem, rsem, offset):
         copy = pltpu.make_async_remote_copy(
@@ -236,6 +236,13 @@
         copy.start()
         return copy
 
+    def store_block(ref, kind, xyz, counts):
+        tiles = xyz.shape[1] // L
+        for a in range(3):
+            for t in range(tiles):
+                ref[kind, pl.ds(a * tiles + t, 1)] = xyz[a:a + 1, t * L:(t + 1) * L]
+        ref[kind, pl.ds(3 * tiles, 1)] = counts
+
     def send_blocks(block, dst, ssem, rsem, kind):
         out = []
         for index, offset in enumerate(peers):
@@ -246,7 +253,7 @@
     staying = code == 13
     keys = bins_of(data)
     for kind in range(3):
-        out3[kind] = sorted_block(data[0:8], keys[kind], staying)
+        store_block(out3, kind, *sorted_block(data[0:8], keys[kind], staying))
     pl.semaphore_wait(barrier, len(peers))
     packets = []
     for index, d in enumerate(DIRS):
@@ -265,7 +272,7 @@
     keys = bins_of(came_t)
     late = []
     for kind in range(3):
-        new3[kind] = sorted_block(came_t[0:8], keys[kind], came_ok)
+        store_block(new3, kind, *sorted_block(came_t[0:8], keys[kind], came_ok))
         late = late + send_blocks(new3, ga_ref, asend, arecv, kind)
     for copy in packets:
         copy.wait_send()
@@ -330,11 +337,14 @@
                 shifts.append(jnp.where(me[axis] == 0, -box, 0.0))
             else:
                 shifts.append(jnp.zeros((1, 1), F32))
+        shift = jnp.concatenate(shifts, axis=0)
         for source, entry in ((gh_ref, index), (ga_ref, index + len(peers))):
-            width = source.shape[2]
+            tiles = source.shape[1] // 3
+            width = tiles * L
             begin = offs_ref[entry, low]
             end = offs_ref[entry, 32 + high]
-            block = jnp.concatenate([source[index, a:a + 1] + shifts[a] for a in range(3)] + [jnp.zeros((5, width), F32)], axis=0)
+            block = jnp.concatenate([source[index, pl.ds(t, 3, stride=tiles), :] for t in range(tiles)], axis=1) + shift
+            block = jnp.concatenate([block, jnp.zeros((5, width), F32)], axis=0)
             block = jnp.concatenate([block, away], axis=1)
             head = fill & (L - 1)
             base = pl.multiple_of(fill - head, L)
@@ -428,23 +438,24 @@
         n = atom_pos.shape[0]
         slots = -(-n // L) * L
         side = jnp.reshape(brick_side, (1, 1))
+        old_rows, new_rows = [3 * (width // L) + 1 for width in (slots, NEW)]
         vmem = pl.BlockSpec(memory_space=pltpu.VMEM)
         smem = pl.BlockSpec(memory_space=pltpu.SMEM)
         srt, ghosts, fresh, own, inner, inner_en = pl.pallas_call(
             functools.partial(exchange_kernel, sizes, peers, slots),
-            out_shape=(jax.ShapeDtypeStruct((16, slots), F32), jax.ShapeDtypeStruct((len(peers), 4, slots), F32), jax.ShapeDtypeStruct((len(peers), 4, NEW), F32),
+            out_shape=(jax.ShapeDtypeStruct((16, slots), F32), jax.ShapeDtypeStruct((len(peers), old_rows, L), F32), jax.ShapeDtypeStruct((len(peers), new_rows, L), F32),
                        jax.ShapeDtypeStruct((slots, 3 * L), F32), jax.ShapeDtypeStruct((3, slots, L), F32), jax.ShapeDtypeStruct((3,) + TILE, F32)),
             in_specs=[pl.BlockSpec(memory_space=pltpu.HBM)] * 5 + [smem],
             out_specs=(vmem,) * 6,
             scratch_shapes=[
                 pltpu.VMEM((3, n), F32), pltpu.VMEM((3, n), F32), pltpu.VMEM((3, n), F32), pltpu.VMEM((n,), I32), pltpu.VMEM((n,), I32),
-                pltpu.VMEM((32, L), F32), pltpu.VMEM((26, L), F32), pltpu.VMEM((3, 4, slots), F32), pltpu.VMEM((3, 4, NEW), F32), pltpu.VMEM((3, 8, CHUNK * L), F32),
+                pltpu.VMEM((32, L), F32), pltpu.VMEM((26, L), F32), pltpu.VMEM((3, old_rows, L), F32), pltpu.VMEM((3, new_rows, L), F32), pltpu.VMEM((3, 8, CHUNK * L), F32),
                 pltpu.SemaphoreType.DMA((5,)), pltpu.SemaphoreType.DMA((26,)), pltpu.SemaphoreType.DMA((26,)),
             ] + [pltpu.SemaphoreType.DMA((len(peers),))] * 4,
             compiler_params=pltpu.CompilerParams(collective_id=0, has_side_effects=True, vmem_limit_bytes=40 * 2 ** 20),
             name="exchange",
         )(*[pltpu.with_memory_space_constraint(v, pltpu.HBM) for v in (atom_pos.T, atom_vel.T, atom_frc.T, atom_id, atom_ok)], side)
-        offs = jnp.concatenate([ghosts[:, 3, 0:64], fresh[:, 3, 0:64]], axis=0).astype(I32)
+        offs = jnp.concatenate([ghosts[:, -1, 0:64], fresh[:, -1, 0:64]], axis=0).astype(I32)
         out_f = jax.ShapeDtypeStruct((3, n), F32)
         out_i = jax.ShapeDtypeStruct((n,), I32)
         new_pos, new_vel, new_frc, new_id, new_ok, energy = pl.pallas_call(

time: 33 us -> 33.3 us (level)
    pallas_call x1, Pallas kernels: 5.29 us -> 6.69 us  [local_step(): pl.pallas_call(functools.partial(force_kernel, sizes, peers, slots), out_...]
    pallas_call x1, Pallas kernels: 9.21 us -> 7.89 us  [local_step(): pl.pallas_call(functools.partial(total_kernel, sizes), out_shape=jax.Shap...]
where the time goes in v1:
time: 33.3 us; the launch traced here: 33 us
  Pallas kernels  31 us (93%)
  between operations  1.33 us (4%)
  other arithmetic  0.61 us (2%)
    pallas_call x1, Pallas kernels, local_step(): pl.pallas_call(functools.partial(exchange_kernel, sizes, peers, slots), o...  16.5 us
    pallas_call x1, Pallas kernels, local_step(): pl.pallas_call(functools.partial(total_kernel, sizes), out_shape=jax.Shap...  7.89 us
    pallas_call x1, Pallas kernels, local_step(): pl.pallas_call(functools.partial(force_kernel, sizes, peers, slots), out_...  6.69 us

profile of v1, /device:TPU:0, one launch (start us, length us, event | category | flops | bytes accessed | tf_op | source)
XLA Modules:
  0.0 33.0 jit_solution(17635178353480646054)
XLA Ops:
  1.3 16.5 %exchange.1 = (f32[16,768]{1,0:T(8,128)S(1)}, f32[17,19,128]{2,1,0:T(8,128)S(1)}, f32[17,7,128]{2,1,0:T(8,128)S(1)}, f32[768,384]{1,0:T(8,128)S(1)}, f32[3,768,1...) custom-call(f32[3,729]{1,0:T(4,128)} %bitcast.12, f32[3,729]{1,0:T(4,128)} %bitcast.13, f32[3,729]{1,0:T(4,128)} %bitcast.14, ...), custom_call_target="tpu_custom_call" | custom-call | tf_op jit(solution)/shard_map/exchange/pallas_call | solution.py:444
  17.8 6.7 %forces.1 = (f32[3,729]{1,0:T(4,128)}, f32[3,729]{1,0:T(4,128)}, f32[3,729]{1,0:T(4,128)}, s32[729]{0:T(1024)}, s32[729]{0:T(1024)}, /*index=5*/f32[1,128]{1,0:T(1,128)S(1)}) custom-call(f32[16,768]{1,0:T(8,128)S(1)} %get-tuple-element.18.srt_ref, f32[17,19,128]{2,1,0:T(8,128)S(1)} %get-tuple-element.19.gh_ref, f32[17,7,128]{2,1,0:T(8,128)S(1)} %get-tuple-element.20.ga_ref, ...), custom_call_target="tpu_custom_call" | custom-call | tf_op jit(solution)/shard_map/forces/pallas_call | solution.py:461
  24.5 7.9 %total.1 = f32[1,128]{1,0:T(1,128)S(1)} custom-call(f32[1,128]{1,0:T(1,128)S(1)} %get-tuple-element.29.part_ref), custom_call_target="tpu_custom_call" | custom-call | tf_op jit(solution)/shard_map/total/pallas_call | solution.py:470
  32.4 0.6 %reduce_sum.9 = f32[]{:T(128)} reduce(f32[1,128]{1,0:T(1,128)S(1)} %total.1, f32[]{:T(128)} %constant.0.clone.1), dimensions={0,1}, to_apply=%region_0.0 | reduce | flops 127 | bytes 520 | tf_op jit(solution)/shard_map/reduce_sum | solution.py:479
  (4 shorter events, 0.1 us)

commit v2 on v1

--- a/solution.py
+++ b/solution.py
@@ -18,7 +18,7 @@
 MAJOR = ((2, 1, 0), (1, 0, 2), (0, 2, 1))
 PACK = 8
 NEW = 256
-CHUNK = 3
+CHUNK = 4
 GROUPS = 8
 L = 128
 TILE = (8, L)

time: 33.3 us -> 33.1 us (level)
  no operation moved by 1% of the time
where the time goes in v2:
time: 33.1 us; the launch traced here: 32.9 us
  Pallas kernels  30.9 us (93%)
  between operations  1.33 us (4%)
  other arithmetic  0.61 us (2%)
    pallas_call x1, Pallas kernels, local_step(): pl.pallas_call(functools.partial(exchange_kernel, sizes, peers, slots), o...  16.5 us
    pallas_call x1, Pallas kernels, local_step(): pl.pallas_call(functools.partial(total_kernel, sizes), out_shape=jax.Shap...  7.89 us
    pallas_call x1, Pallas kernels, local_step(): pl.pallas_call(functools.partial(force_kernel, sizes, peers, slots), out_...  6.59 us

profile of v2, /device:TPU:0, one launch (start us, length us, event | category | flops | bytes accessed | tf_op | source)
XLA Modules:
  0.0 32.9 jit_solution(16225065066294143272)
XLA Ops:
  1.3 16.5 %exchange.1 = (f32[16,768]{1,0:T(8,128)S(1)}, f32[17,19,128]{2,1,0:T(8,128)S(1)}, f32[17,7,128]{2,1,0:T(8,128)S(1)}, f32[768,384]{1,0:T(8,128)S(1)}, f32[3,768,1...) custom-call(f32[3,729]{1,0:T(4,128)} %bitcast.12, f32[3,729]{1,0:T(4,128)} %bitcast.13, f32[3,729]{1,0:T(4,128)} %bitcast.14, ...), custom_call_target="tpu_custom_call" | custom-call | tf_op jit(solution)/shard_map/exchange/pallas_call | solution.py:444
  17.8 6.6 %forces.1 = (f32[3,729]{1,0:T(4,128)}, f32[3,729]{1,0:T(4,128)}, f32[3,729]{1,0:T(4,128)}, s32[729]{0:T(1024)}, s32[729]{0:T(1024)}, /*index=5*/f32[1,128]{1,0:T(1,128)S(1)}) custom-call(f32[16,768]{1,0:T(8,128)S(1)} %get-tuple-element.18.srt_ref, f32[17,19,128]{2,1,0:T(8,128)S(1)} %get-tuple-element.19.gh_ref, f32[17,7,128]{2,1,0:T(8,128)S(1)} %get-tuple-element.20.ga_ref, ...), custom_call_target="tpu_custom_call" | custom-call | tf_op jit(solution)/shard_map/forces/pallas_call | solution.py:461
  24.4 7.9 %total.1 = f32[1,128]{1,0:T(1,128)S(1)} custom-call(f32[1,128]{1,0:T(1,128)S(1)} %get-tuple-element.29.part_ref), custom_call_target="tpu_custom_call" | custom-call | tf_op jit(solution)/shard_map/total/pallas_call | solution.py:470
  32.3 0.6 %reduce_sum.9 = f32[]{:T(128)} reduce(f32[1,128]{1,0:T(1,128)S(1)} %total.1, f32[]{:T(128)} %constant.0.clone.1), dimensions={0,1}, to_apply=%region_0.0 | reduce | flops 127 | bytes 520 | tf_op jit(solution)/shard_map/reduce_sum | solution.py:479
  (4 shorter events, 0.1 us)

commit v3 on v2

--- a/solution.py
+++ b/solution.py
@@ -250,17 +250,16 @@
                 out.append(send(block.at[kind], dst.at[index], ssem.at[index], rsem.at[index], offset))
         return out
 
-    staying = code == 13
-    keys = bins_of(data)
-    for kind in range(3):
-        store_block(out3, kind, *sorted_block(data[0:8], keys[kind], staying))
     pl.semaphore_wait(barrier, len(peers))
     packets = []
     for index, d in enumerate(DIRS):
         row = pl.ds(index, 1)
         packets.append(send(pkt.at[row], rcv.at[row], psend.at[index], precv.at[index], offset_of(sizes, d)))
     blocks = []
+    staying = code == 13
+    keys = bins_of(data)
     for kind in range(3):
+        store_block(out3, kind, *sorted_block(data[0:8], keys[kind], staying))
         blocks = blocks + send_blocks(out3, gh_ref, gsend, grecv, kind)
     for copy in packets:
         copy.wait_recv()

time: 33.1 us -> 33.4 us (level)
  no operation moved by 1% of the time
where the time goes in v3:
time: 33.4 us; the launch traced here: 33.2 us
  Pallas kernels  31.2 us (93%)
  between operations  1.33 us (4%)
  other arithmetic  0.61 us (2%)
    pallas_call x1, Pallas kernels, local_step(): pl.pallas_call(functools.partial(exchange_kernel, sizes, peers, slots), o...  16.7 us
    pallas_call x1, Pallas kernels, local_step(): pl.pallas_call(functools.partial(total_kernel, sizes), out_shape=jax.Shap...  7.89 us
    pallas_call x1, Pallas kernels, local_step(): pl.pallas_call(functools.partial(force_kernel, sizes, peers, slots), out_...  6.59 us

profile of v3, /device:TPU:0, one launch (start us, length us, event | category | flops | bytes accessed | tf_op | source)
XLA Modules:
  0.0 33.2 jit_solution(351620561706450538)
XLA Ops:
  1.3 16.7 %exchange.1 = (f32[16,768]{1,0:T(8,128)S(1)}, f32[17,19,128]{2,1,0:T(8,128)S(1)}, f32[17,7,128]{2,1,0:T(8,128)S(1)}, f32[768,384]{1,0:T(8,128)S(1)}, f32[3,768,1...) custom-call(f32[3,729]{1,0:T(4,128)} %bitcast.12, f32[3,729]{1,0:T(4,128)} %bitcast.13, f32[3,729]{1,0:T(4,128)} %bitcast.14, ...), custom_call_target="tpu_custom_call" | custom-call | tf_op jit(solution)/shard_map/exchange/pallas_call | solution.py:443
  18.1 6.6 %forces.1 = (f32[3,729]{1,0:T(4,128)}, f32[3,729]{1,0:T(4,128)}, f32[3,729]{1,0:T(4,128)}, s32[729]{0:T(1024)}, s32[729]{0:T(1024)}, /*index=5*/f32[1,128]{1,0:T(1,128)S(1)}) custom-call(f32[16,768]{1,0:T(8,128)S(1)} %get-tuple-element.18.srt_ref, f32[17,19,128]{2,1,0:T(8,128)S(1)} %get-tuple-element.19.gh_ref, f32[17,7,128]{2,1,0:T(8,128)S(1)} %get-tuple-element.20.ga_ref, ...), custom_call_target="tpu_custom_call" | custom-call | tf_op jit(solution)/shard_map/forces/pallas_call | solution.py:460
  24.7 7.9 %total.1 = f32[1,128]{1,0:T(1,128)S(1)} custom-call(f32[1,128]{1,0:T(1,128)S(1)} %get-tuple-element.29.part_ref), custom_call_target="tpu_custom_call" | custom-call | tf_op jit(solution)/shard_map/total/pallas_call | solution.py:469
  32.6 0.6 %reduce_sum.9 = f32[]{:T(128)} reduce(f32[1,128]{1,0:T(1,128)S(1)} %total.1, f32[]{:T(128)} %constant.0.clone.1), dimensions={0,1}, to_apply=%region_0.0 | reduce | flops 127 | bytes 520 | tf_op jit(solution)/shard_map/reduce_sum | solution.py:478
  (4 shorter events, 0.1 us)

commit v4 on v2

--- a/solution.py
+++ b/solution.py
@@ -35,6 +35,10 @@
 
 def offset_of(sizes, d):
     return tuple(c % size for c, size in zip(d, sizes))
+
+
+def far_first(d):
+    return sum(c == 0 for c in d)
 
 
 def order_of(d):
@@ -167,7 +171,7 @@
         load.start()
         loads.append(load)
     barrier = pltpu.get_barrier_semaphore()
-    for offset in peers:
+    for offset in sorted(peers, key=far_first):
         pl.semaphore_signal(barrier, inc=1, device_id=device_at(offset), device_id_type=pl.DeviceIdType.MESH)
 
     n = pos_ref.shape[1]
@@ -245,7 +249,8 @@
 
     def send_blocks(block, dst, ssem, rsem, kind):
         out = []
-        for index, offset in enumerate(peers):
+        for offset in sorted(peers, key=far_first):
+            index = peers.index(offset)
             if order_of(tuple(0 if c == 0 else 1 for c in offset)) == kind:
                 out.append(send(block.at[kind], dst.at[index], ssem.at[index], rsem.at[index], offset))
         return out
@@ -256,7 +261,8 @@
         store_block(out3, kind, *sorted_block(data[0:8], keys[kind], staying))
     pl.semaphore_wait(barrier, len(peers))
     packets = []
-    for index, d in enumerate(DIRS):
+    for d in sorted(DIRS, key=far_first):
+        index = DIRS.index(d)
         row = pl.ds(index, 1)
         packets.append(send(pkt.at[row], rcv.at[row], psend.at[index], precv.at[index], offset_of(sizes, d)))
     blocks = []

time: 33.1 us -> 33.2 us (level)
  no operation moved by 1% of the time
where the time goes in v4:
time: 33.2 us; the launch traced here: 33 us
  Pallas kernels  31 us (93%)
  between operations  1.33 us (4%)
  other arithmetic  0.61 us (2%)
    pallas_call x1, Pallas kernels, local_step(): pl.pallas_call(functools.partial(exchange_kernel, sizes, peers, slots), o...  16.5 us
    pallas_call x1, Pallas kernels, local_step(): pl.pallas_call(functools.partial(total_kernel, sizes), out_shape=jax.Shap...  7.91 us
    pallas_call x1, Pallas kernels, local_step(): pl.pallas_call(functools.partial(force_kernel, sizes, peers, slots), out_...  6.6 us

profile of v4, /device:TPU:0, one launch (start us, length us, event | category | flops | bytes accessed | tf_op | source)
XLA Modules:
  0.0 33.0 jit_solution(8502928098738424314)
XLA Ops:
  1.3 16.5 %exchange.1 = (f32[16,768]{1,0:T(8,128)S(1)}, f32[17,19,128]{2,1,0:T(8,128)S(1)}, f32[17,7,128]{2,1,0:T(8,128)S(1)}, f32[768,384]{1,0:T(8,128)S(1)}, f32[3,768,1...) custom-call(f32[3,729]{1,0:T(4,128)} %bitcast.12, f32[3,729]{1,0:T(4,128)} %bitcast.13, f32[3,729]{1,0:T(4,128)} %bitcast.14, ...), custom_call_target="tpu_custom_call" | custom-call | tf_op jit(solution)/shard_map/exchange/pallas_call | solution.py:450
  17.9 6.6 %forces.1 = (f32[3,729]{1,0:T(4,128)}, f32[3,729]{1,0:T(4,128)}, f32[3,729]{1,0:T(4,128)}, s32[729]{0:T(1024)}, s32[729]{0:T(1024)}, /*index=5*/f32[1,128]{1,0:T(1,128)S(1)}) custom-call(f32[16,768]{1,0:T(8,128)S(1)} %get-tuple-element.18.srt_ref, f32[17,19,128]{2,1,0:T(8,128)S(1)} %get-tuple-element.19.gh_ref, f32[17,7,128]{2,1,0:T(8,128)S(1)} %get-tuple-element.20.ga_ref, ...), custom_call_target="tpu_custom_call" | custom-call | tf_op jit(solution)/shard_map/forces/pallas_call | solution.py:467
  24.5 7.9 %total.1 = f32[1,128]{1,0:T(1,128)S(1)} custom-call(f32[1,128]{1,0:T(1,128)S(1)} %get-tuple-element.29.part_ref), custom_call_target="tpu_custom_call" | custom-call | tf_op jit(solution)/shard_map/total/pallas_call | solution.py:476
  32.4 0.6 %reduce_sum.9 = f32[]{:T(128)} reduce(f32[1,128]{1,0:T(1,128)S(1)} %total.1, f32[]{:T(128)} %constant.0.clone.1), dimensions={0,1}, to_apply=%region_0.0 | reduce | flops 127 | bytes 520 | tf_op jit(solution)/shard_map/reduce_sum | solution.py:485
  (4 shorter events, 0.1 us)

commit v5 on v4

--- a/solution.py
+++ b/solution.py
@@ -376,13 +376,14 @@
 
     def own_step(q, energy):
         start = tuple(tuple(inner_ref[a, step_rows(q, g), :] for a in range(3)) for g in range(GROUPS))
-        carry = pair_loop(own_cols, wide_line, q, 0, 1, True, (start, energy))
-        force, energy = pair_loop(own_cols, wide_line, q, 1, chunks, False, carry)
+        carry = pair_loop(own_cols, wide_line, q, 0, own_chunks, True, (start, energy))
+        force, energy = pair_loop(own_cols, wide_line, q, own_chunks, chunks, False, carry)
         for g in range(GROUPS):
             for a in range(3):
                 sums[a, step_rows(q, g), :] = force[g][a]
         return energy
 
+    own_chunks = jnp.where(count > first, 1, 0)
     own_steps = (count + 8 * GROUPS - 1) // (8 * GROUPS)
     energy = lax.fori_loop(0, own_steps, own_step, tuple(inner_en_ref[k] for k in range(3)))
     en_ref[...] = jnp.sum(2.0 * energy[0] - 12.0 * energy[1] + 0.5 * (RC * UPC - UCUT) * energy[2], axis=0, keepdims=True)

time: 33.2 us -> 32.8 us (0.988); the launches traced: 33 us -> 33.1 us
  no operation moved by 1% of the time
where the time goes in v5:
time: 32.8 us; the launch traced here: 33.1 us
  Pallas kernels  31.1 us (95%)
  between operations  1.33 us (4%)
  other arithmetic  0.61 us (2%)
    pallas_call x1, Pallas kernels, local_step(): pl.pallas_call(functools.partial(exchange_kernel, sizes, peers, slots), o...  16.5 us
    pallas_call x1, Pallas kernels, local_step(): pl.pallas_call(functools.partial(total_kernel, sizes), out_shape=jax.Shap...  7.89 us
    pallas_call x1, Pallas kernels, local_step(): pl.pallas_call(functools.partial(force_kernel, sizes, peers, slots), out_...  6.67 us

profile of v5, /device:TPU:0, one launch (start us, length us, event | category | flops | bytes accessed | tf_op | source)
XLA Modules:
  0.0 33.1 jit_solution(8002976866145352186)
XLA Ops:
  1.3 16.5 %exchange.1 = (f32[16,768]{1,0:T(8,128)S(1)}, f32[17,19,128]{2,1,0:T(8,128)S(1)}, f32[17,7,128]{2,1,0:T(8,128)S(1)}, f32[768,384]{1,0:T(8,128)S(1)}, f32[3,768,1...) custom-call(f32[3,729]{1,0:T(4,128)} %bitcast.12, f32[3,729]{1,0:T(4,128)} %bitcast.13, f32[3,729]{1,0:T(4,128)} %bitcast.14, ...), custom_call_target="tpu_custom_call" | custom-call | tf_op jit(solution)/shard_map/exchange/pallas_call | solution.py:451
  17.9 6.7 %forces.1 = (f32[3,729]{1,0:T(4,128)}, f32[3,729]{1,0:T(4,128)}, f32[3,729]{1,0:T(4,128)}, s32[729]{0:T(1024)}, s32[729]{0:T(1024)}, /*index=5*/f32[1,128]{1,0:T(1,128)S(1)}) custom-call(f32[16,768]{1,0:T(8,128)S(1)} %get-tuple-element.18.srt_ref, f32[17,19,128]{2,1,0:T(8,128)S(1)} %get-tuple-element.19.gh_ref, f32[17,7,128]{2,1,0:T(8,128)S(1)} %get-tuple-element.20.ga_ref, ...), custom_call_target="tpu_custom_call" | custom-call | tf_op jit(solution)/shard_map/forces/pallas_call | solution.py:468
  24.6 7.9 %total.1 = f32[1,128]{1,0:T(1,128)S(1)} custom-call(f32[1,128]{1,0:T(1,128)S(1)} %get-tuple-element.29.part_ref), custom_call_target="tpu_custom_call" | custom-call | tf_op jit(solution)/shard_map/total/pallas_call | solution.py:477
  32.5 0.6 %reduce_sum.9 = f32[]{:T(128)} reduce(f32[1,128]{1,0:T(1,128)S(1)} %total.1, f32[]{:T(128)} %constant.0.clone.1), dimensions={0,1}, to_apply=%region_0.0 | reduce | flops 127 | bytes 520 | tf_op jit(solution)/shard_map/reduce_sum | solution.py:486
  (4 shorter events, 0.1 us)
